TPU v7x, 512 devices: a whole 4x8x8 slice. The times are simulated.
512 devices in a mesh: blk: 32 (over z, y_lo), head: 16 (over x, y_hi, core).
Axes of the slice: x: 4, y: 8 (y_hi: 2, y_lo: 4; y = y_hi * 4 + y_lo), z: 8, core: 2. Of those that a mesh axis runs over, the one named last changes fastest.
Arguments:
- queries: bfloat16 [16384, 1024], P('blk', 'head'), may hold values from -170 to 170
- key_rows: bfloat16 [16384, 1024], P('blk', 'head'), may hold values from -9 to 9
- values: bfloat16 [16384, 1024], P('blk', 'head'), may hold values from -48 to 48
- text_keys: bfloat16 [1232, 1024], P(None, 'head'), may hold values from -9 to 9
- text_values: bfloat16 [1232, 1024], P(None, 'head'), may hold values from -48 to 48
- block_image: int32 [128], replicated, may hold values from 0 to 7, as said below
- gate_image: float32 [8, 1536], replicated, may hold values from 0.5 to 2
- residual: bfloat16 [16384, 1536], P(('blk', 'head')), may hold values from -6 to 6
- w_out: bfloat16 [1024, 1536], P('head'), may hold values from -0.1875 to 0.1875
Outputs:
- stream_out: bfloat16 [16384, 1536], P(('blk', 'head'))
Inputs may be any that keep to these rules, and one draw needn't show every extreme that they name: `block_image`: each image number 0 to 7 names 8 to 24 of the entries, some image exactly 24 and some exactly 8; the blocks of an image lie anywhere in the array.
All inputs are finite; a program needn't handle non-finite values.
Results may differ from a plain program's by a relative error of at most 0.014.
Values may be sent and summed in bfloat16 or wider, within the bound.
A program may use at most 64 MiB of HBM per device.

v0:
```python
import math
import jax
import jax.numpy as jnp
from jax import lax
from jax.sharding import PartitionSpec as P

HD = 64
TEXT = 154
BS = 128
neg_large = -1e30


def side_by_side(arrays, axis, dim, along):
    widths = [a.shape[along] for a in arrays]
    both = jnp.concatenate(arrays, axis=along)
    result = lax.all_gather(both, axis, axis=dim, tiled=True)
    return tuple(jnp.split(result, [sum(widths[:k]) for k in range(1, len(widths))], axis=along))


def absorb(running, query_three, query_image, key_slab, value_slab, key_image):
    best, total, accum = running
    heads = query_three.shape[1]
    width = query_three.shape[2]
    key_three = key_slab.reshape(key_slab.shape[0], heads, width)
    value_three = value_slab.reshape(value_slab.shape[0], heads, width)
    scores = jnp.einsum("qhd,khd->hqk", query_three, key_three, preferred_element_type=jnp.float32)
    scores = scores * (1.0 / math.sqrt(width))
    allowed = query_image[:, None] == key_image[None, :]
    scores = jnp.where(allowed[None], scores, neg_large)
    newbest = jnp.maximum(best, jnp.max(scores, axis=2))
    weights = jnp.exp(scores - newbest[..., None])
    shrink = jnp.exp(best - newbest)
    total = total * shrink + jnp.sum(weights, axis=2)
    update = jnp.einsum(
        "hqk,khd->hqd",
        weights.astype(jnp.bfloat16),
        value_three,
        preferred_element_type=jnp.float32,
    )
    accum = accum * shrink[..., None] + update
    return (newbest, total, accum)


def on_device(
    queries, key_rows, values, text_keys, text_values, block_image, gate_image, residual, w_out
):
    tok_blk = queries.shape[0]
    ncols = queries.shape[1]
    heads_here = ncols // HD
    blocks_here = tok_blk // BS
    token_image = jnp.repeat(block_image, BS)
    blk_index = lax.axis_index("blk")
    my_blocks = lax.dynamic_slice_in_dim(block_image, blk_index * blocks_here, blocks_here)
    query_image = jnp.repeat(my_blocks, BS)
    text_image = jnp.arange(text_keys.shape[0]) // TEXT
    start_state = (
        jnp.full((heads_here, tok_blk), neg_large, jnp.float32),
        jnp.zeros((heads_here, tok_blk), jnp.float32),
        jnp.zeros((heads_here, tok_blk, HD), jnp.float32),
    )
    query_three = queries.reshape(tok_blk, heads_here, HD)
    running = absorb(start_state, query_three, query_image, text_keys, text_values, text_image)
    fold_running = running
    key_piece, value_piece = side_by_side((key_rows, values), "blk", 0, 1)
    length = key_piece.shape[0]

    def advance(state, position):
        begin = position * tok_blk
        key_slab = lax.dynamic_slice_in_dim(key_piece, begin, tok_blk)
        value_slab = lax.dynamic_slice_in_dim(value_piece, begin, tok_blk)
        slab_image = lax.dynamic_slice_in_dim(token_image, begin, tok_blk)
        return (absorb(state, query_three, query_image, key_slab, value_slab, slab_image), None)

    fold_running, unused = lax.scan(
        advance, fold_running, jnp.arange(length // tok_blk, dtype=jnp.int32)
    )
    best, total, accum = fold_running
    attended = (accum / total[..., None]).astype(jnp.bfloat16)
    attended = attended.transpose(1, 0, 2).reshape(tok_blk, ncols)
    tok_dev = tok_blk // lax.axis_size("head")
    mixed = lax.all_to_all(attended, "head", split_axis=0, concat_axis=1, tiled=True)
    projected = jnp.dot(
        mixed, lax.all_gather(w_out, "head", axis=0, tiled=True), preferred_element_type=jnp.float32
    )
    head_index = lax.axis_index("head")
    row_image = lax.dynamic_slice_in_dim(query_image, head_index * tok_dev, tok_dev)
    onehot = (
        row_image[:, None] == jnp.arange(gate_image.shape[0], dtype=jnp.int32)[None, :]
    ).astype(jnp.float32)
    gating = jnp.dot(onehot, gate_image, precision=lax.Precision.HIGHEST)
    return (residual.astype(jnp.float32) + gating * projected).astype(jnp.bfloat16)


def solution(mesh):
    placed = (
        P("blk", "head"),
        P("blk", "head"),
        P("blk", "head"),
        P(None, "head"),
        P(None, "head"),
        P(),
        P(),
        P(("blk", "head"), None),
        P("head", None),
    )
    return jax.shard_map(
        on_device, mesh=mesh, in_specs=placed, out_specs=P(("blk", "head"), None), check_vma=False
    )
```

profile of v0, /device:TPU:1, one launch (start us, length us, event | category | flops | bytes accessed | tf_op | source)
XLA Modules:
  0.0 353.7 jit_solution(8619565113360705211)
XLA Ops:
  11.6 1.5 fusion.35
  14.2 148.3 %all-gather.3.cloned.1.call-done = bf16[16384,128]{1,0:T(8,128)(2,1)} async-done(((bf16[512,128]{1,0:T(8,128)(2,1)}), bf16[16384,128]{1,0:T(8,128)(2,1)}) %all-gather.3.cloned.1.call-update) | async-done | bytes 4194320 | tf_op jit(solution)/shard_map/all_gather | solution.py:16
  162.5 7.3 %fusion.34 = (bf16[16384,64]{1,0:T(8,128)(2,1)}, bf16[16384,64]{1,0:T(8,128)(2,1)}) fusion(bf16[16384,128]{1,0:T(8,128)(2,1)} %all-gather.3.cloned.1.call-done), kind=kLoop, calls=%fused_computation.48 | loop fusion | bytes 8388608 | tf_op jit(solution)/shard_map/split | solution.py:17
  169.9 133.4 %while.15 = (s32[]{:T(128)}, f32[1,512]{1,0:T(1,128)S(1)}, f32[1,512]{1,0:T(1,128)S(1)}, f32[1,512,64]{1,2,0:T(8,128)S(1)}, s32[32]{0:T(128)S(1)}, /*index=5*/s3...) while((s32[]{:T(128)}, f32[1,512]{1,0:T(1,128)S(1)}, ...), condition=%wide.region_5.6_spmd.clone, body=%wide.region_2.5_spmd.clone.sunk | while | flops 69272576 | bytes 3778779 | solution.py:74
  172.8 1.2 fusion.51
  181.1 1.2 fusion.51
  185.3 1.2 fusion.51
  189.4 1.2 fusion.51
  197.8 1.2 fusion.51
  201.9 1.2 fusion.51
  206.1 1.2 fusion.51
  210.3 1.2 fusion.51
  214.4 1.2 fusion.51
  218.6 1.2 fusion.51
  226.9 1.2 fusion.51
  231.1 1.2 fusion.51
  243.6 1.2 fusion.51
  247.8 1.2 fusion.51
  252.0 1.3 fusion.51
  260.3 1.2 fusion.51
  281.2 1.2 fusion.51
  304.3 29.3 %all-to-all-start = ((bf16[16,2,1024]{2,1,0:T(2,128)(2,1)}), bf16[16,2,1024]{2,1,0:T(2,128)(2,1)S(1)}, u32[]{:S(2)}, u32[]{:S(2)}) async-start(bf16[16,2,1024]{2,1,0:T(2,128)(2,1)} %reshape.134), calls=%async_computation | async-start | bytes 131072 | tf_op jit(solution)/shard_map/all_to_all | solution.py:81
  333.8 9.4 %all-to-all-done = bf16[16,2,1024]{2,1,0:T(2,128)(2,1)S(1)} async-done(((bf16[16,2,1024]{2,1,0:T(2,128)(2,1)}), bf16[16,2,1024]{2,1,0:T(2,128)(2,1)S(1)}, u32[]{:S(2)}, u32[]{:S(2)}) %all-to-all-start) | async-done | bytes 65568 | tf_op jit(solution)/shard_map/all_to_all | solution.py:81
  343.7 3.2 fusion.16
  (306 shorter events, 97.0 us)
Async XLA Ops:
  6.5 5.1 %copy-start = (bf16[1232,64]{0,1:T(8,128)(2,1)S(1)}, bf16[1232,64]{0,1:T(8,128)(2,1)}, u32[]{:S(2)}) copy-start(bf16[1232,64]{0,1:T(8,128)(2,1)} %param.14) | copy-start | bytes 473092
  6.5 155.9 %all-gather.3.cloned.1.call-start = ((), (), s32[]{:S(2)}) async-start(), calls=%async_computation.1 | async-start | bytes 4325376 | tf_op jit(solution)/shard_map/all_gather | solution.py:16
  9.3 334.4 %all-gather.5.cloned.1.call-start = ((), (), s32[]{:S(2)}) async-start(), calls=%async_computation.2 | async-start | bytes 3342336 | tf_op jit(solution)/shard_map/all_gather | solution.py:83
  11.6 2.0 copy-start.1
  14.2 155.6 %copy-start.4 = (bf16[512,64]{0,1:T(8,128)(2,1)S(1)}, bf16[512,64]{0,1:T(8,128)(2,1)}, u32[]{:S(2)}) copy-start(bf16[512,64]{0,1:T(8,128)(2,1)} %param.11) | copy-start | bytes 196612
  169.8 163.7 %copy-start.3 = (f32[8,1536]{1,0:T(8,128)S(1)}, f32[8,1536]{1,0:T(8,128)}, u32[]{:S(2)}) copy-start(f32[8,1536]{1,0:T(8,128)} %param.17) | copy-start | bytes 147460
  169.8 173.8 %copy-start.2 = (bf16[32,1536]{1,0:T(8,128)(2,1)S(1)}, bf16[32,1536]{1,0:T(8,128)(2,1)}, u32[]{:S(2)}) copy-start(bf16[32,1536]{1,0:T(8,128)(2,1)} %param.18) | copy-start | bytes 294916
  304.3 39.0 %all-to-all-start = ((bf16[16,2,1024]{2,1,0:T(2,128)(2,1)}), bf16[16,2,1024]{2,1,0:T(2,128)(2,1)S(1)}, u32[]{:S(2)}, u32[]{:S(2)}) async-start(bf16[16,2,1024]{2,1,0:T(2,128)(2,1)} %reshape.134), calls=%async_computation | async-start | bytes 131072 | tf_op jit(solution)/shard_map/all_to_all | solution.py:81
Sparse Core Ops, SparseCore 0:
  9.4 153.0 all-gather.2
  165.8 94.2 all-gather.4
where the time goes:
time: 355 us; the launch traced here: 354 us
  waiting for transfers between devices  158 us (45%)
  matrix products  83 us (23%)
  local copies, waits for them, and re-layouts  37.7 us (11%)
  starting transfers between devices  29.3 us (8%)
  loops' own time  23.2 us (7%)
  between operations  13.5 us (4%)
  other arithmetic  8.42 us (2%)
    all_gather x1, waiting for transfers between devices, side_by_side(): result = lax.all_gather(both, axis, axis=dim, tiled=True)  148 us
    dot_general x33, matrix products, absorb(): jnp.einsum('qhd,khd->hqk', query_three, key_three, preferred_element_type...  39.8 us
    dot_general x33, matrix products, absorb(): jnp.einsum('hqk,khd->hqd', weights.astype(jnp.bfloat16), value_three, pre...  39.7 us
    all_to_all x1, starting transfers between devices, on_device(): lax.all_to_all(attended, 'head', split_axis=0, concat_axis=1, tiled=True)  29.3 us
    another operation x1, loops' own time, on_device(): lax.scan(advance, fold_running, jnp.arange(length // tok_blk, dtype=jnp.i...  23.2 us
    dynamic_slice x32, local copies, waits for them, and re-layouts, on_device(): lax.scan(advance, fold_running, jnp.arange(length // tok_blk, dtype=jnp.i...  20.8 us
    all_to_all x1, waiting for transfers between devices, on_device(): lax.all_to_all(attended, 'head', split_axis=0, concat_axis=1, tiled=True)  9.44 us
    split x1, local copies, waits for them, and re-layouts, side_by_side(): jnp.split(result, [sum(widths[:k]) for k in range(1, len(widths))], axis=...  7.34 us
  transfers between devices with their start and end apart: 3, of which 2 were waited for; matrix products, arithmetic and copies ran while one was open for 35% of the time, Pallas kernels for 0%

commit v1 on v0

--- a/solution.py
+++ b/solution.py
@@ -78,7 +78,9 @@
     attended = (accum / total[..., None]).astype(jnp.bfloat16)
     attended = attended.transpose(1, 0, 2).reshape(tok_blk, ncols)
     tok_dev = tok_blk // lax.axis_size("head")
-    mixed = lax.all_to_all(attended, "head", split_axis=0, concat_axis=1, tiled=True)
+    pieces = jnp.split(attended, lax.axis_size("head"), axis=0)
+    arrived = lax.all_to_all(jnp.stack(pieces), "head", 0, 0)
+    mixed = jnp.concatenate(arrived, axis=1)
     projected = jnp.dot(
         mixed, lax.all_gather(w_out, "head", axis=0, tiled=True), preferred_element_type=jnp.float32
     )

time: 355 us -> 356 us (level)
  no operation moved by 1% of the time
where the time goes in v1:
time: 356 us; the launch traced here: 354 us
  waiting for transfers between devices  158 us (44%)
  matrix products  83 us (23%)
  local copies, waits for them, and re-layouts  37.9 us (11%)
  starting transfers between devices  29.3 us (8%)
  loops' own time  23.2 us (7%)
  between operations  13.6 us (4%)
  other arithmetic  8.42 us (2%)
    all_gather x1, waiting for transfers between devices, side_by_side(): result = lax.all_gather(both, axis, axis=dim, tiled=True)  148 us
    dot_general x33, matrix products, absorb(): jnp.einsum('qhd,khd->hqk', query_three, key_three, preferred_element_type...  39.8 us
    dot_general x33, matrix products, absorb(): jnp.einsum('hqk,khd->hqd', weights.astype(jnp.bfloat16), value_three, pre...  39.7 us
    all_to_all x1, starting transfers between devices, on_device(): arrived = lax.all_to_all(jnp.stack(pieces), 'head', 0, 0)  29.3 us
    another operation x1, loops' own time, on_device(): lax.scan(advance, fold_running, jnp.arange(length // tok_blk, dtype=jnp.i...  23.2 us
    dynamic_slice x32, local copies, waits for them, and re-layouts, on_device(): lax.scan(advance, fold_running, jnp.arange(length // tok_blk, dtype=jnp.i...  20.8 us
    all_to_all x1, waiting for transfers between devices, on_device(): arrived = lax.all_to_all(jnp.stack(pieces), 'head', 0, 0)  9.44 us
    split x1, local copies, waits for them, and re-layouts, side_by_side(): jnp.split(result, [sum(widths[:k]) for k in range(1, len(widths))], axis=...  7.34 us
  transfers between devices with their start and end apart: 3, of which 2 were waited for; matrix products, arithmetic and copies ran while one was open for 35% of the time, Pallas kernels for 0%

profile of v1, /device:TPU:1, one launch (start us, length us, event | category | flops | bytes accessed | tf_op | source)
XLA Modules:
  0.0 353.9 jit_solution(5157665660335921528)
XLA Ops:
  11.6 1.5 fusion.35
  14.2 148.3 %all-gather.3.cloned.1.call-done = bf16[16384,128]{1,0:T(8,128)(2,1)} async-done(((bf16[512,128]{1,0:T(8,128)(2,1)}), bf16[16384,128]{1,0:T(8,128)(2,1)}) %all-gather.3.cloned.1.call-update) | async-done | bytes 4194320 | tf_op jit(solution)/shard_map/all_gather | solution.py:16
  162.5 7.3 %fusion.34 = (bf16[16384,64]{1,0:T(8,128)(2,1)}, bf16[16384,64]{1,0:T(8,128)(2,1)}) fusion(bf16[16384,128]{1,0:T(8,128)(2,1)} %all-gather.3.cloned.1.call-done), kind=kLoop, calls=%fused_computation.64 | loop fusion | bytes 8388608 | tf_op jit(solution)/shard_map/split | solution.py:17
  169.9 133.4 %while.15 = (s32[]{:T(128)}, f32[1,512]{1,0:T(1,128)S(1)}, f32[1,512]{1,0:T(1,128)S(1)}, f32[1,512,64]{1,2,0:T(8,128)S(1)}, s32[32]{0:T(128)S(1)}, /*index=5*/s3...) while((s32[]{:T(128)}, f32[1,512]{1,0:T(1,128)S(1)}, ...), condition=%wide.region_5.6_spmd.clone, body=%wide.region_2.5_spmd.clone.sunk | while | flops 69272576 | bytes 3778779 | solution.py:74
  172.8 1.2 fusion.51
  181.1 1.2 fusion.51
  185.3 1.2 fusion.51
  189.4 1.2 fusion.51
  197.8 1.2 fusion.51
  201.9 1.2 fusion.51
  206.1 1.2 fusion.51
  210.3 1.2 fusion.51
  214.4 1.2 fusion.51
  218.6 1.2 fusion.51
  226.9 1.2 fusion.51
  231.1 1.2 fusion.51
  243.6 1.2 fusion.51
  247.8 1.2 fusion.51
  252.0 1.3 fusion.51
  260.3 1.2 fusion.51
  281.2 1.2 fusion.51
  304.5 29.3 %all-to-all-start = ((bf16[16,2,1024]{2,1,0:T(2,128)(2,1)}), bf16[16,2,1024]{2,1,0:T(2,128)(2,1)S(1)}, u32[]{:S(2)}, u32[]{:S(2)}) async-start(bf16[16,2,1024]{2,1,0:T(2,128)(2,1)} %reshape.170), calls=%async_computation | async-start | bytes 131072 | tf_op jit(solution)/shard_map/all_to_all | solution.py:82
  334.0 9.4 %all-to-all-done = bf16[16,2,1024]{2,1,0:T(2,128)(2,1)S(1)} async-done(((bf16[16,2,1024]{2,1,0:T(2,128)(2,1)}), bf16[16,2,1024]{2,1,0:T(2,128)(2,1)S(1)}, u32[]{:S(2)}, u32[]{:S(2)}) %all-to-all-start) | async-done | bytes 65568 | tf_op jit(solution)/shard_map/all_to_all | solution.py:82
  343.9 3.2 fusion.16
  (322 shorter events, 97.2 us)
Async XLA Ops:
  6.5 5.1 %copy-start = (bf16[1232,64]{0,1:T(8,128)(2,1)S(1)}, bf16[1232,64]{0,1:T(8,128)(2,1)}, u32[]{:S(2)}) copy-start(bf16[1232,64]{0,1:T(8,128)(2,1)} %param.14) | copy-start | bytes 473092
  6.5 155.9 %all-gather.3.cloned.1.call-start = ((), (), s32[]{:S(2)}) async-start(), calls=%async_computation.1 | async-start | bytes 4325376 | tf_op jit(solution)/shard_map/all_gather | solution.py:16
  9.3 334.5 %all-gather.5.cloned.1.call-start = ((), (), s32[]{:S(2)}) async-start(), calls=%async_computation.2 | async-start | bytes 3342336 | tf_op jit(solution)/shard_map/all_gather | solution.py:85
  11.6 2.0 copy-start.1
  14.2 155.6 %copy-start.4 = (bf16[512,64]{0,1:T(8,128)(2,1)S(1)}, bf16[512,64]{0,1:T(8,128)(2,1)}, u32[]{:S(2)}) copy-start(bf16[512,64]{0,1:T(8,128)(2,1)} %param.11) | copy-start | bytes 196612
  169.8 163.9 %copy-start.3 = (f32[8,1536]{1,0:T(8,128)S(1)}, f32[8,1536]{1,0:T(8,128)}, u32[]{:S(2)}) copy-start(f32[8,1536]{1,0:T(8,128)} %param.17) | copy-start | bytes 147460
  169.8 174.0 %copy-start.2 = (bf16[32,1536]{1,0:T(8,128)(2,1)S(1)}, bf16[32,1536]{1,0:T(8,128)(2,1)}, u32[]{:S(2)}) copy-start(bf16[32,1536]{1,0:T(8,128)(2,1)} %param.18) | copy-start | bytes 294916
  304.5 39.0 %all-to-all-start = ((bf16[16,2,1024]{2,1,0:T(2,128)(2,1)}), bf16[16,2,1024]{2,1,0:T(2,128)(2,1)S(1)}, u32[]{:S(2)}, u32[]{:S(2)}) async-start(bf16[16,2,1024]{2,1,0:T(2,128)(2,1)} %reshape.170), calls=%async_computation | async-start | bytes 131072 | tf_op jit(solution)/shard_map/all_to_all | solution.py:82
Sparse Core Ops, SparseCore 0:
  9.4 153.0 all-gather.2
  165.8 94.2 all-gather.4
